TPU v7x, 32 devices: a whole 2x2x4 slice. The times are simulated.
32 devices in a mesh: doc: 8 (over y, x, core), seg: 4 (over z).
Axes of the slice: x: 2, y: 2, z: 4, core: 2. Of those that a mesh axis runs over, the one named last changes fastest.
Arguments:
- tokens: int32 [2048], P(('doc', 'seg')), parts along dimension 0, may hold values from 0 to 20479
- targets: int32 [2048], P(('doc', 'seg')), parts along dimension 0, may hold values from 0 to 20479
- embedding: bfloat16 [20480, 1024], P('seg'), may hold values from -2 to 2
- qkv_weight: bfloat16 [2, 1024, 3, 1024], P(None, None, None, 'seg'), may hold values from -2 to 2
- pos_weight: bfloat16 [2, 1024, 1024], P(None, None, 'seg'), may hold values from -0.375 to 0.375
- out_weight: bfloat16 [2, 1024, 1024], P(None, None, 'seg'), may hold values from -0.1875 to 0.1875
- content_bias: float32 [2, 1024], replicated, may hold values from -3 to 3
- position_bias: float32 [2, 1024], replicated, may hold values from -6 to 6
- norm_gain: float32 [2, 1024], replicated, may hold values from 0.25 to 8
- norm_shift: float32 [2, 1024], replicated, may hold values from -2 to 2
Outputs:
- token_loglik: float32 [2048], P(('doc', 'seg')), parts along dimension 0
- doc_mean: float32 [8], P('doc'), parts along dimension 0
There are 8 independent parts, one for each index of `doc`. A program takes and returns all parts, laid end to end along the dimension named above; an argument that names none is the same for every part. Nothing has to cross between parts.
All inputs are finite; a program needn't handle non-finite values.
Results may differ from a plain program's by a relative error of at most 0.005.
The roundings to bfloat16 on the way count: a program that leaves them out, or rounds other values in their place, can miss the bound.
Values may be sent and summed in bfloat16 or wider, within the bound.
A program may use at most 128 MiB of HBM per device.

v0:
```python
import math

import jax
import jax.numpy as jnp
from jax import lax
from jax.sharding import PartitionSpec as P

HEADS = 16
MEM_SEGS = 6
LAYERS = 2


def merged(shard, axis, combine):
    everything = jax.tree.map(lambda part: lax.all_gather(part, axis), shard)
    initial = jax.tree.map(lambda part: part[0], everything)

    def hop(k, so_far):
        return combine(so_far, jax.tree.map(lambda part: part[k], everything))

    return lax.fori_loop(1, lax.axis_size(axis), hop, initial)


def layer_norm(total, gain, shift):
    middle = jnp.mean(total, axis=-1, keepdims=True)
    spread = jnp.mean(jnp.square(total - middle), axis=-1, keepdims=True)
    return ((total - middle) / jnp.sqrt(spread + 1e-05) * gain + shift).astype(jnp.bfloat16)


def position_table(key_len, model_width):
    places = (key_len - 1 - jnp.arange(key_len)).astype(jnp.float32)
    inverse = jnp.power(10000.0, -jnp.arange(0, model_width, 2).astype(jnp.float32) / model_width)
    angles = places[:, None] * inverse[None, :]
    return jnp.concatenate([jnp.sin(angles), jnp.cos(angles)], axis=1).astype(jnp.bfloat16)


def relative_shift(raw_position, query_len, key_len):
    head_count = raw_position.shape[0]
    padded = jnp.pad(raw_position, ((0, 0), (0, 0), (0, 1)))
    flattened = padded.reshape(head_count, query_len * (key_len + 1))
    shifted = lax.slice_in_dim(
        flattened, query_len - 1, query_len - 1 + query_len * key_len, axis=1
    )
    return shifted.reshape(head_count, query_len, key_len)


def attend(with_content, with_position, key_heads, value_heads, pos_heads, visible, head_dim):
    query_len = with_content.shape[0]
    key_len = key_heads.shape[0]
    content = jnp.einsum(
        "thd,khd->htk", with_content, key_heads, preferred_element_type=jnp.float32
    )
    raw_position = jnp.einsum(
        "thd,khd->htk", with_position, pos_heads, preferred_element_type=jnp.float32
    )
    shifted = relative_shift(raw_position, query_len, key_len)
    scores = (content + shifted) * (1.0 / math.sqrt(head_dim))
    scores = jnp.where(visible[None], scores, jnp.float32(-1e30))
    row_max = jnp.max(scores, axis=2, keepdims=True)
    weights = jnp.exp(scores - row_max)
    attn_probs = (weights / jnp.sum(weights, axis=2, keepdims=True)).astype(jnp.bfloat16)
    head_mix = jnp.einsum(
        "htk,khd->thd", attn_probs, value_heads, preferred_element_type=jnp.float32
    )
    return head_mix.astype(jnp.bfloat16).reshape(query_len, with_content.shape[1] * head_dim)


def head_attention(layer_input, qkv_local, pos_local, u_row, v_row, head_dim):
    seg_len = layer_input.shape[0]
    model_width = layer_input.shape[1]
    group_size = lax.axis_size("seg")
    columns = qkv_local.shape[2]
    head_count = columns // head_dim
    mem_len = MEM_SEGS * seg_len
    first_column = lax.axis_index("seg") * columns
    matrix = qkv_local.reshape(model_width, 3 * columns)
    piece = lax.all_gather(layer_input, "seg", axis=0, tiled=True)
    product = jnp.dot(piece, matrix, preferred_element_type=jnp.float32)
    project = product.astype(jnp.bfloat16).reshape(piece.shape[0], 3, columns)
    total_rows = project.shape[0]
    block_segs = min(group_size, max(1, 512 // seg_len))
    while group_size % block_segs != 0:
        block_segs -= 1
    block_len = block_segs * seg_len
    key_span = mem_len + block_len
    block_count = group_size // block_segs
    pos_table = position_table(key_span, model_width)
    pos_keys = jnp.dot(pos_table, pos_local, preferred_element_type=jnp.float32).astype(
        jnp.bfloat16
    )
    pos_heads = pos_keys.reshape(key_span, head_count, head_dim)
    queries = project[:, 0, :].astype(jnp.float32)
    u_part = lax.dynamic_slice_in_dim(u_row, first_column, columns, 0)
    v_part = lax.dynamic_slice_in_dim(v_row, first_column, columns, 0)
    with_content = (queries + u_part).astype(jnp.bfloat16).reshape(total_rows, head_count, head_dim)
    with_position = (
        (queries + v_part).astype(jnp.bfloat16).reshape(total_rows, head_count, head_dim)
    )
    padded_kv = jnp.concatenate(
        [jnp.zeros((mem_len, 2, columns), jnp.bfloat16), project[:, 1:, :]], axis=0
    )
    row_ids = jnp.arange(block_len)[:, None]
    col_ids = jnp.arange(key_span)[None, :]

    def one_block(block_at):
        start = block_at * block_len
        block_content = lax.dynamic_slice_in_dim(with_content, start, block_len, 0)
        block_position = lax.dynamic_slice_in_dim(with_position, start, block_len, 0)
        window = lax.dynamic_slice_in_dim(padded_kv, start, key_span, 0)
        key_heads = window[:, 0, :].reshape(key_span, head_count, head_dim)
        value_heads = window[:, 1, :].reshape(key_span, head_count, head_dim)
        query_place = start + row_ids
        key_place = start - mem_len + col_ids
        visible = (key_place <= query_place) & (key_place >= 0)
        visible = visible & (key_place >= query_place // seg_len * seg_len - mem_len)
        return attend(
            block_content, block_position, key_heads, value_heads, pos_heads, visible, head_dim
        )

    mixed = lax.map(one_block, jnp.arange(block_count, dtype=jnp.int32)).reshape(
        total_rows, columns
    )
    return lax.all_to_all(mixed, "seg", split_axis=0, concat_axis=1, tiled=True)


def combine_words(first, second):
    top = jnp.maximum(first[0], second[0])
    total = first[1] * jnp.exp(first[0] - top) + second[1] * jnp.exp(second[0] - top)
    return (top, total, first[2] + second[2])


def on_device(
    tokens,
    targets,
    embedding,
    qkv_weight,
    pos_weight,
    out_weight,
    content_bias,
    position_bias,
    norm_gain,
    norm_shift,
):
    seg_len = tokens.shape[0]
    model_width = embedding.shape[1]
    vocab_rows = embedding.shape[0]
    head_dim = model_width // HEADS
    seg_index = lax.axis_index("seg")
    group_size = lax.axis_size("seg")
    first_word = seg_index * vocab_rows
    all_tokens, all_targets = (
        lax.all_gather(tokens, "seg", axis=0, tiled=True),
        lax.all_gather(targets, "seg", axis=0, tiled=True),
    )
    local_ids = all_tokens - first_word
    inside = (local_ids >= 0) & (local_ids < vocab_rows)
    rows = jnp.take(embedding, jnp.clip(local_ids, 0, vocab_rows - 1), axis=0)
    looked = lax.psum_scatter(
        jnp.where(inside[:, None], rows.astype(jnp.float32), 0.0).astype(jnp.bfloat16),
        "seg",
        scatter_dimension=0,
        tiled=True,
    ).astype(jnp.float32)
    hidden = (looked * math.sqrt(model_width)).astype(jnp.bfloat16)
    for layer_at in range(LAYERS):
        layer_input = hidden
        head_mix = head_attention(
            layer_input,
            qkv_weight[layer_at],
            pos_weight[layer_at],
            content_bias[layer_at],
            position_bias[layer_at],
            head_dim,
        )
        attended = jnp.dot(
            head_mix,
            lax.all_gather(out_weight[layer_at], "seg", axis=1, tiled=True),
            preferred_element_type=jnp.float32,
        )
        hidden = layer_norm(
            layer_input.astype(jnp.float32) + attended, norm_gain[layer_at], norm_shift[layer_at]
        )
    word_ids = first_word + jnp.arange(vocab_rows)[None, :]
    logits = jnp.einsum(
        "td,vd->tv",
        lax.all_gather(hidden, "seg", axis=0, tiled=True),
        embedding,
        preferred_element_type=jnp.float32,
    )
    piece_max = jnp.max(logits, axis=1)
    piece_sum = jnp.sum(jnp.exp(logits - piece_max[:, None]), axis=1)
    piece_pick = jnp.sum(jnp.where(word_ids == all_targets[:, None], logits, 0.0), axis=1)
    top, total, picked = merged((piece_max, piece_sum, piece_pick), "seg", combine_words)
    own_start = seg_index * seg_len
    own_top = lax.dynamic_slice_in_dim(top, own_start, seg_len, 0)
    own_total = lax.dynamic_slice_in_dim(total, own_start, seg_len, 0)
    own_pick = lax.dynamic_slice_in_dim(picked, own_start, seg_len, 0)
    token_loglik = own_pick - (jnp.log(own_total) + own_top)
    grand_total = lax.psum(jnp.sum(token_loglik), "seg")
    doc_mean = (grand_total / (seg_len * group_size)).reshape(1)
    return (token_loglik, doc_mean)


def solution(mesh):
    in_specs = (
        P(("doc", "seg")),
        P(("doc", "seg")),
        P("seg", None),
        P(None, None, None, "seg"),
        P(None, None, "seg"),
        P(None, None, "seg"),
        P(),
        P(),
        P(),
        P(),
    )
    out_specs = (P(("doc", "seg")), P("doc"))
    return jax.shard_map(
        on_device, mesh=mesh, in_specs=in_specs, out_specs=out_specs, check_vma=False
    )
```

profile of v0, /device:TPU:0, one launch (start us, length us, event | category | flops | bytes accessed | tf_op | source)
XLA Modules:
  0.0 229.4 jit_solution(3143187229040833979)
XLA Ops:
  7.2 1.2 dynamic-slice.4
  9.1 0.9 dynamic-update-slice
  10.0 0.8 dynamic-update-slice.1
  10.8 9.9 %all-reduce.6 = (s32[256]{0:T(256)S(1)}, s32[256]{0:T(256)S(1)}) all-reduce(s32[256]{0:T(256)S(1)} %dynamic-update-slice, s32[256]{0:T(256)S(1)} %dynamic-update-slice.1), channel_id=1, replica_groups=mesh['doc'=8,'seg'=4] {'seg'}, use_global_device_ids=true, to_apply=%add.4 | all-reduce | flops 512 | bytes 4096
  20.8 7.0 %gather_fusion = bf16[256,1024]{1,0:T(8,128)(2,1)S(1)} fusion(bf16[5120,1024]{1,0:T(8,128)(2,1)} %param.14, s32[1024]{0:T(1024)S(1)} %pad_clamp_fusion), kind=kCustom, calls=%fused_computation | custom fusion | bytes 1049600 | tf_op jit(solution)/shard_map/jit(_take)/gather | solution.py:156
  27.8 1.0 select_convert_fusion
  28.9 1.1 fusion.52
  30.0 0.7 all-gather.13.cloned.1.call-update
  30.8 5.1 %fusion.10 = (bf16[640,512]{1,0:T(8,128)(2,1)S(1)}, bf16[640,512]{1,0:T(8,128)(2,1)S(1)}) fusion(f32[512]{0:T(512)S(1)} %multiply_power_fusion, f32[640]{0:T(1024)S(1)} %subtract_convert_fusion), kind=kLoop, calls=%fused_computation.25 | loop fusion | flops 983040 | bytes 1315328 | tf_op jit(solution)/shard_map/convert.2
  35.9 1.4 convolution_convert_fusion.3
  37.3 1.4 convolution_convert_fusion.2
  39.3 1.4 fusion.51
  40.7 0.9 copy.39
  42.0 8.0 %reduce-scatter.2.cloned.1.call-done = bf16[64,1024]{1,0:T(8,128)(2,1)} async-done(((bf16[256,1024]{1,0:T(8,128)(2,1)}), bf16[64,1024]{1,0:T(8,128)(2,1)}) %reduce-scatter.2.cloned.1.call-update) | async-done | bytes 131088 | tf_op jit(solution)/shard_map/reduce_scatter | solution.py:157
  50.1 0.9 multiply_convert_fusion
  51.0 18.4 %all_gather.40 = bf16[256,1024]{1,0:T(8,128)(2,1)S(1)} all-gather(bf16[64,1024]{1,0:T(8,128)(2,1)S(1)} %multiply_convert_fusion), channel_id=1, replica_groups=mesh['doc'=8,'seg'=4] {'seg'}, dimensions={0}, use_global_device_ids=true | all-gather | bytes 655360 | tf_op jit(solution)/shard_map/all_gather | solution.py:76
  70.3 0.7 slice.122
  71.9 4.4 %reshape.260 = f32[4,164096]{1,0:T(4,128)} reshape(f32[4,256,641]{2,1,0:T(8,128)S(1)} %pad.11) | data formatting | bytes 5251072 | tf_op jit(solution)/shard_map/while/body/eval_jaxpr/reshape | solution.py:39
  76.3 2.9 %slice.124 = f32[4,163840]{1,0:T(4,128)S(1)} slice(f32[4,164096]{1,0:T(4,128)} %reshape.260), slice={[0:4], [255:164095]} | slice | bytes 5242880 | tf_op jit(solution)/shard_map/while/body/eval_jaxpr/slice | solution.py:40
  79.2 0.8 pad_slice_fusion.2
  80.0 0.8 fusion.5
  81.8 2.0 fusion.22
  84.0 0.8 copy.34
  84.9 3.6 %all-to-all-start = ((bf16[4,64,256]{2,1,0:T(8,128)(2,1)}), bf16[4,64,256]{2,1,0:T(8,128)(2,1)S(1)}, u32[]{:S(2)}, u32[]{:S(2)}) async-start(bf16[4,64,256]{2,1,0:T(8,128)(2,1)} %copy.34), calls=%async_computation.1 | async-start | bytes 262144 | tf_op jit(solution)/shard_map/all_to_all | solution.py:122
  88.4 1.7 copy.40
  90.3 8.2 %all-to-all-done = bf16[4,64,256]{2,1,0:T(8,128)(2,1)S(1)} async-done(((bf16[4,64,256]{2,1,0:T(8,128)(2,1)}), bf16[4,64,256]{2,1,0:T(8,128)(2,1)S(1)}, u32[]{:S(2)}, u32[]{:S(2)}) %all-to-all-start) | async-done | bytes 131104 | tf_op jit(solution)/shard_map/all_to_all | solution.py:122
  98.6 4.3 %all-gather.11.cloned.1.call-done = bf16[1,1024,1024]{2,1,0:T(8,128)(2,1)} async-done(((bf16[1,1024,256]{2,1,0:T(8,128)(2,1)}), bf16[1,1024,1024]{2,1,0:T(8,128)(2,1)}) %all-gather.11.cloned.1.call-update) | async-done | bytes 2097168 | tf_op jit(solution)/shard_map/all_gather | solution.py:176
  102.9 2.2 fusion.58
  105.4 25.0 %all_gather.42 = bf16[256,1024]{1,0:T(8,128)(2,1)S(1)} all-gather(bf16[64,1024]{1,0:T(8,128)(2,1)S(1)} %add_convert_fusion.1), channel_id=1, replica_groups=mesh['doc'=8,'seg'=4] {'seg'}, dimensions={0}, use_global_device_ids=true | all-gather | bytes 655360 | tf_op jit(solution)/shard_map/all_gather | solution.py:76
  131.2 0.7 slice.125
  132.9 4.5 %reshape.264 = f32[4,164096]{1,0:T(4,128)} reshape(f32[4,256,641]{2,1,0:T(8,128)S(1)} %pad.12) | data formatting | bytes 5251072 | tf_op jit(solution)/shard_map/while/body/eval_jaxpr/reshape | solution.py:39
  137.4 2.9 %slice.127 = f32[4,163840]{1,0:T(4,128)S(1)} slice(f32[4,164096]{1,0:T(4,128)} %reshape.264), slice={[0:4], [255:164095]} | slice | bytes 5242880 | tf_op jit(solution)/shard_map/while/body/eval_jaxpr/slice | solution.py:40
  140.3 0.8 pad_slice_fusion
  141.0 0.8 fusion.3
  142.9 2.0 fusion.23
  145.1 0.8 copy.35
  145.9 3.3 %all-to-all-start.1 = ((bf16[4,64,256]{2,1,0:T(8,128)(2,1)}), bf16[4,64,256]{2,1,0:T(8,128)(2,1)S(1)}, u32[]{:S(2)}, u32[]{:S(2)}) async-start(bf16[4,64,256]{2,1,0:T(8,128)(2,1)} %copy.35), calls=%async_computation.2 | async-start | bytes 262144 | tf_op jit(solution)/shard_map/all_to_all | solution.py:122
  149.2 7.3 %all-to-all-done.1 = bf16[4,64,256]{2,1,0:T(8,128)(2,1)S(1)} async-done(((bf16[4,64,256]{2,1,0:T(8,128)(2,1)}), bf16[4,64,256]{2,1,0:T(8,128)(2,1)S(1)}, u32[]{:S(2)}, u32[]{:S(2)}) %all-to-all-start.1) | async-done | bytes 131104 | tf_op jit(solution)/shard_map/all_to_all | solution.py:122
  156.5 1.4 all-gather.13.cloned.1.call-done
  157.9 2.2 fusion.60
  160.4 15.9 %all_gather.44 = bf16[256,1024]{1,0:T(8,128)(2,1)S(1)} all-gather(bf16[64,1024]{1,0:T(8,128)(2,1)S(1)} %add_convert_fusion), channel_id=1, replica_groups=mesh['doc'=8,'seg'=4] {'seg'}, dimensions={0}, use_global_device_ids=true | all-gather | bytes 655360 | tf_op jit(solution)/shard_map/all_gather | solution.py:185
  176.3 5.9 %fusion.61 = (f32[256]{0:T(256)S(1)}, f32[256,5120]{1,0:T(8,128)S(1)}) fusion(bf16[256,1024]{1,0:T(8,128)(2,1)S(1)} %all_gather.44, bf16[5120,1024]{1,0:T(8,128)(2,1)} %param.14), kind=kOutput, calls=%fused_computation.113 | convolution fusion | flops 2685665024 | bytes 16253952 | tf_op jit(solution)/shard_map/td,vd->tv/dot_general | solution.py:183
  182.2 1.7 select_reduce_fusion
  183.9 7.6 %all-gather.6 = f32[4,1,256]{2,1,0:T(1,128)S(1)} all-gather(f32[1,1,256]{2,1,0:T(1,128)S(1)} %bitcast.147), channel_id=5, replica_groups=mesh['doc'=8,'seg'=4] {'seg'}, dimensions={0}, use_global_device_ids=true | all-gather | bytes 5120 | tf_op jit(solution)/shard_map/all_gather | solution.py:14
  191.5 9.6 %all-gather.7 = f32[4,1,256]{2,1,0:T(1,128)S(1)} all-gather(f32[1,1,256]{2,1,0:T(1,128)S(1)} %bitcast.146), channel_id=6, replica_groups=mesh['doc'=8,'seg'=4] {'seg'}, dimensions={0}, use_global_device_ids=true | all-gather | bytes 5120 | tf_op jit(solution)/shard_map/all_gather | solution.py:14
  201.1 7.6 %all-gather.5 = f32[4,1,256]{2,1,0:T(1,128)S(1)} all-gather(f32[1,1,256]{2,1,0:T(1,128)S(1)} %bitcast.145), channel_id=4, replica_groups=mesh['doc'=8,'seg'=4] {'seg'}, dimensions={0}, use_global_device_ids=true | all-gather | bytes 5120 | tf_op jit(solution)/shard_map/all_gather | solution.py:14
  208.9 1.2 fusion.50
  210.1 11.0 %psum.7 = f32[]{:T(128)} all-reduce(f32[]{:T(128)} %get-tuple-element.251), channel_id=1, replica_groups=mesh['doc'=8,'seg'=4] {'seg'}, use_global_device_ids=true, to_apply=%region_15.16 | all-reduce | flops 1 | bytes 8 | tf_op jit(solution)/shard_map/psum | solution.py:198
  (101 shorter events, 8.2 us)
Async XLA Ops:
  7.2 42.9 %reduce-scatter.2.cloned.1.call-start = ((), (), s32[]{:S(2)}) async-start(), calls=%async_computation.3 | async-start | bytes 655360 | tf_op jit(solution)/shard_map/reduce_scatter | solution.py:157
  20.8 8.1 %copy-start.5 = (bf16[2,1024,256]{2,1,0:T(8,128)(2,1)S(1)}, bf16[2,1024,256]{2,1,0:T(8,128)(2,1)}, u32[]{:S(2)}) copy-start(bf16[2,1024,256]{2,1,0:T(8,128)(2,1)} %param.17) | copy-start | bytes 3145732
  28.8 7.1 %copy-start.15 = (bf16[2,1024,256]{2,1,0:T(8,128)(2,1)S(1)}, bf16[2,1024,256]{2,1,0:T(8,128)(2,1)}, u32[]{:S(2)}) copy-start(bf16[2,1024,256]{2,1,0:T(8,128)(2,1)} %param.16) | copy-start | bytes 3145732
  28.8 74.1 %all-gather.11.cloned.1.call-start = ((), (), s32[]{:S(2)}) async-start(), calls=%async_computation.4 | async-start | bytes 2621440 | tf_op jit(solution)/shard_map/all_gather | solution.py:176
  30.0 127.9 %all-gather.13.cloned.1.call-start = ((), (), s32[]{:S(2)}) async-start(), calls=%async_computation.5 | async-start | bytes 2621440 | tf_op jit(solution)/shard_map/all_gather | solution.py:176
  37.3 2.0 copy-start
  40.7 0.9 copy-start.11
  40.7 0.9 copy-start.12
  40.7 1.1 copy-start.13
  41.8 29.2 %copy-start.10 = (bf16[640,256]{0,1:T(8,128)(2,1)S(1)}, bf16[640,256]{0,1:T(8,128)(2,1)}, u32[]{:S(2)}) copy-start(bf16[640,256]{0,1:T(8,128)(2,1)} %convolution_convert_fusion.3) | copy-start | bytes 983044
  76.3 2.9 %copy-start.4 = (bf16[256,2,256]{0,2,1:T(8,128)(2,1)S(1)}, bf16[256,2,256]{0,2,1:T(8,128)(2,1)}, u32[]{:S(2)}) copy-start(bf16[256,2,256]{0,2,1:T(8,128)(2,1)} %slice.122) | copy-start | bytes 786436
  80.8 1.0 copy-start.8
  81.8 6.6 %copy-start.14 = (f32[2,1024]{1,0:T(2,128)S(1)}, f32[2,1024]{1,0:T(2,128)}, u32[]{:S(2)}) copy-start(f32[2,1024]{1,0:T(2,128)} %param.21) | copy-start | bytes 24580
  83.9 19.0 %copy-start.6 = (bf16[64,1024]{1,0:T(8,128)(2,1)S(1)}, bf16[64,1024]{1,0:T(8,128)(2,1)}, u32[]{:S(2)}) copy-start(bf16[64,1024]{1,0:T(8,128)(2,1)} %reduce-scatter.2.cloned.1.call-done) | copy-start | bytes 393220
  84.9 13.7 %all-to-all-start = ((bf16[4,64,256]{2,1,0:T(8,128)(2,1)}), bf16[4,64,256]{2,1,0:T(8,128)(2,1)S(1)}, u32[]{:S(2)}, u32[]{:S(2)}) async-start(bf16[4,64,256]{2,1,0:T(8,128)(2,1)} %copy.34), calls=%async_computation.1 | async-start | bytes 262144 | tf_op jit(solution)/shard_map/all_to_all | solution.py:122
  105.3 26.7 %copy-start.9 = (bf16[640,256]{0,1:T(8,128)(2,1)S(1)}, bf16[640,256]{0,1:T(8,128)(2,1)}, u32[]{:S(2)}) copy-start(bf16[640,256]{0,1:T(8,128)(2,1)} %convolution_convert_fusion.2) | copy-start | bytes 983044
  131.2 0.8 copy-start.1
  137.4 2.9 %copy-start.3 = (bf16[256,2,256]{0,2,1:T(8,128)(2,1)S(1)}, bf16[256,2,256]{0,2,1:T(8,128)(2,1)}, u32[]{:S(2)}) copy-start(bf16[256,2,256]{0,2,1:T(8,128)(2,1)} %slice.125) | copy-start | bytes 786436
  137.4 3.7 %copy-start.2 = (bf16[256,1,256]{0,2,1:T(8,128)(2,1)S(1)}, bf16[256,1,256]{0,2,1:T(8,128)(2,1)}, u32[]{:S(2)}) copy-start(bf16[256,1,256]{0,2,1:T(8,128)(2,1)} %copy-done.1) | copy-start | bytes 393220
  141.9 1.0 copy-start.7
  145.9 10.6 %all-to-all-start.1 = ((bf16[4,64,256]{2,1,0:T(8,128)(2,1)}), bf16[4,64,256]{2,1,0:T(8,128)(2,1)S(1)}, u32[]{:S(2)}, u32[]{:S(2)}) async-start(bf16[4,64,256]{2,1,0:T(8,128)(2,1)} %copy.35), calls=%async_computation.2 | async-start | bytes 262144 | tf_op jit(solution)/shard_map/all_to_all | solution.py:122
Sparse Core Ops, SparseCore 0:
  28.9 21.0 reduce-scatter.1
  51.6 51.2 all-gather.10
  104.5 53.3 all-gather.12
where the time goes:
time: 230 us; the launch traced here: 229 us
  blocking collectives  105 us (46%)
  local copies, waits for them, and re-layouts  37.2 us (16%)
  waiting for transfers between devices  29.9 us (13%)
  matrix products  21.2 us (9%)
  between operations  16.6 us (7%)
  other arithmetic  12.3 us (5%)
  starting transfers between devices  7.01 us (3%)
    all_gather x2, blocking collectives, head_attention(): piece = lax.all_gather(layer_input, 'seg', axis=0, tiled=True)  43.4 us
    all_gather x3, blocking collectives, merged(): everything = jax.tree.map(lambda part: lax.all_gather(part, axis), shard)  24.7 us
    all_gather x1, blocking collectives, on_device(): lax.all_gather(hidden, 'seg', axis=0, tiled=True)  15.9 us
    all_to_all x2, waiting for transfers between devices, head_attention(): return lax.all_to_all(mixed, 'seg', split_axis=0, concat_axis=1, tiled=True)  15.5 us
    psum x1, blocking collectives, on_device(): grand_total = lax.psum(jnp.sum(token_loglik), 'seg')  11 us
    unnamed x1, blocking collectives  9.92 us
    reshape x2, local copies, waits for them, and re-layouts, relative_shift(): flattened = padded.reshape(head_count, query_len * (key_len + 1))  8.92 us
    reduce_scatter x1, waiting for transfers between devices, on_device(): lax.psum_scatter(jnp.where(inside[:, None], rows.astype(jnp.float32), 0.0...  8.05 us
  transfers between devices with their start and end apart: 5, of which 5 were waited for; matrix products, arithmetic and copies ran while one was open for 21% of the time, Pallas kernels for 0%

commit v1 on v0

--- a/solution.py
+++ b/solution.py
@@ -1,8 +1,11 @@
+import functools
 import math
 
 import jax
 import jax.numpy as jnp
 from jax import lax
+from jax.experimental import pallas as pl
+from jax.experimental.pallas import tpu as pltpu
 from jax.sharding import PartitionSpec as P
 
 HEADS = 16
@@ -200,6 +203,432 @@
     return (token_loglik, doc_mean)
 
 
+MESH = pl.DeviceIdType.MESH
+EPS = 1e-05
+
+
+def mega_kernel(
+    n, docs, seg_len, mem_len, head_dim,
+    ids_ref, emb_hbm, qkv_hbm, pos_hbm, out_hbm, cb_ref, pb_ref, ng_ref, ns_ref,
+    lo_sin, lo_cos, hi_sin, hi_cos,
+    row_out, mean_out,
+    emb, qkv, posw, wfull, idbuf, onehot, gsend, rsbuf, hid, table, pkeys, mixg, stats, xres,
+    emb_sem, w_sem, p_sem, o_sem,
+    id_s, id_r, rs_s, rs_r, ag_s, ag_r, w1_s, w1_r, w2_s, w2_r, w3_s, w3_r, mx_s, mx_r, st_s, st_r,
+):
+    layers = qkv.shape[0]
+    total = n * seg_len
+    vocab, width = emb.shape
+    cols = width // n
+    chunks = hid.shape[0]
+    cw = hid.shape[2]
+    per = width // docs
+    me = lax.axis_index("seg")
+    doc = lax.axis_index("doc")
+    pairs = docs // 2
+    core = lax.rem(doc, 2)
+    chip = doc // 2
+    partner = chip * 2 + 1 - core
+
+    def seg_peer(k):
+        return (doc, lax.rem(me + k, n))
+
+    def plane_peer(j):
+        return (lax.rem(chip + j, pairs) * 2 + core, me)
+
+    def remote(src, dst, send, recv, device):
+        return pltpu.make_async_remote_copy(
+            src_ref=src, dst_ref=dst, send_sem=send, recv_sem=recv,
+            device_id=device, device_id_type=MESH,
+        )
+
+    emb_copies = [
+        pltpu.make_async_copy(
+            emb_hbm.at[:, c * cw : (c + 1) * cw], emb.at[:, c * cw : (c + 1) * cw], emb_sem.at[c]
+        )
+        for c in range(chunks)
+    ]
+    out_copies = [
+        pltpu.make_async_copy(out_hbm.at[l], wfull.at[l, me], o_sem.at[l]) for l in range(layers)
+    ]
+    pos_copy = pltpu.make_async_copy(pos_hbm, posw, p_sem)
+    qkv_copy = pltpu.make_async_copy(qkv_hbm, qkv, w_sem)
+    out_copies[0].start()
+    emb_copies[0].start()
+    for copy in emb_copies[1:]:
+        copy.start()
+    for copy in out_copies[1:]:
+        copy.start()
+    pos_copy.start()
+    qkv_copy.start()
+
+    barrier = pltpu.get_barrier_semaphore()
+    friends = [seg_peer(k) for k in range(1, n)] + [plane_peer(j) for j in range(1, pairs)]
+    friends.append((partner, me))
+    for friend in friends:
+        pl.semaphore_signal(barrier, inc=1, device_id=friend, device_id_type=MESH)
+    pl.semaphore_wait(barrier, len(friends))
+
+    id_copies = [
+        remote(ids_ref, idbuf.at[k - 1], id_s.at[k - 1], id_r.at[k - 1], seg_peer(k))
+        for k in range(1, n)
+    ]
+    for copy in id_copies:
+        copy.start()
+
+    mine = pl.ds(pl.multiple_of(doc * per, per), per)
+
+    def w1(l):
+        return [
+            remote(
+                wfull.at[l, me, mine], wfull.at[l, me, mine], w1_s.at[l, k - 1],
+                w1_r.at[l, k - 1], seg_peer(k),
+            )
+            for k in range(1, n)
+        ]
+
+    w1_copies = [w1(l) for l in range(layers)]
+    out_copies[0].wait()
+    for copy in w1_copies[0]:
+        copy.start()
+
+    def w2(l):
+        found = []
+        for k in range(1, n):
+            src = lax.rem(me - k + n, n)
+            for j in range(1, pairs):
+                ref = wfull.at[l, src, mine]
+                found.append(
+                    remote(ref, ref, w2_s.at[l, k - 1, j - 1], w2_r.at[l, k - 1, j - 1], plane_peer(j))
+                )
+        return found
+
+    def w3(l):
+        found = []
+        for k in range(1, n):
+            src = lax.rem(me - k + n, n)
+            for j in range(pairs):
+                owner = lax.rem(chip - j + pairs, pairs) * 2 + core
+                ref = wfull.at[l, src, pl.ds(pl.multiple_of(owner * per, per), per)]
+                found.append(
+                    remote(ref, ref, w3_s.at[l, k - 1, j], w3_r.at[l, k - 1, j], (partner, me))
+                )
+        return found
+
+    w2_copies = [w2(l) for l in range(layers)]
+    w3_copies = [w3(l) for l in range(layers)]
+
+    eye = lax.broadcasted_iota(jnp.int32, (2 * seg_len, 2 * seg_len), 0) == lax.broadcasted_iota(
+        jnp.int32, (2 * seg_len, 2 * seg_len), 1
+    )
+
+    def column(row):
+        return jnp.sum(jnp.where(eye, row, 0), axis=1, keepdims=True)
+
+    for copy in id_copies:
+        copy.wait_recv()
+    idbuf[n - 1] = ids_ref[...]
+    first_word = me * vocab
+    tok_cols = []
+    tgt_cols = []
+    for s in range(n):
+        slot = lax.rem(me - s + 2 * n - 1, n)
+        both = column(idbuf[slot, 0:1, :]) - first_word
+        tok_cols.append(both[:seg_len])
+        tgt_cols.append(both[seg_len:])
+    tokens = jnp.concatenate(tok_cols, axis=0)
+    targets = jnp.concatenate(tgt_cols, axis=0)
+    wb = 512
+    for v in range(vocab // wb):
+        words = lax.broadcasted_iota(jnp.int32, (total, wb), 1) + v * wb
+        onehot[:, v * wb : (v + 1) * wb] = (tokens == words).astype(jnp.float32).astype(jnp.bfloat16)
+
+    def rows_of(s):
+        return pl.ds(pl.multiple_of(s * seg_len, seg_len), seg_len)
+
+    rs_copies = []
+    for c in range(chunks):
+        emb_copies[c].wait()
+        gsend[c] = jnp.dot(
+            onehot[...], emb[:, c * cw : (c + 1) * cw], preferred_element_type=jnp.float32
+        ).astype(jnp.bfloat16)
+        group = []
+        for k in range(1, n):
+            peer = lax.rem(me + k, n)
+            copy = remote(
+                gsend.at[c, rows_of(peer)], rsbuf.at[c, k - 1], rs_s.at[c, k - 1],
+                rs_r.at[c, k - 1], (doc, peer),
+            )
+            copy.start()
+            group.append(copy)
+        rs_copies.append(group)
+
+    for copy in w1_copies[0]:
+        copy.wait_recv()
+    for copy in w2_copies[0]:
+        copy.start()
+    out_copies[1].wait()
+
+    step = lo_sin.shape[0]
+    half = width // 2
+    for a in range(total // step):
+        hs = hi_sin[a : a + 1, :]
+        hc = hi_cos[a : a + 1, :]
+        rows = slice(a * step, (a + 1) * step)
+        table[rows, :half] = (hs * lo_cos[...] + hc * lo_sin[...]).astype(jnp.bfloat16)
+        table[rows, half:] = (hc * lo_cos[...] - hs * lo_sin[...]).astype(jnp.bfloat16)
+
+    ag_copies = []
+    for c in range(chunks):
+        for copy in rs_copies[c]:
+            copy.wait_recv()
+        own = gsend[c, rows_of(me), :].astype(jnp.float32)
+        for k in range(1, n):
+            own = own + rsbuf[c, k - 1].astype(jnp.float32)
+        hid[c, rows_of(me), :] = (own * math.sqrt(width)).astype(jnp.bfloat16)
+        group = []
+        for k in range(1, n):
+            ref = hid.at[c, rows_of(me)]
+            copy = remote(ref, ref, ag_s.at[c, k - 1], ag_r.at[c, k - 1], seg_peer(k))
+            copy.start()
+            group.append(copy)
+        ag_copies.append(group)
+
+    for l in range(1, layers):
+        for copy in w1_copies[l]:
+            copy.start()
+
+    pos_copy.wait()
+    for l in range(layers):
+        pkeys[l] = jnp.dot(table[...], posw[l], preferred_element_type=jnp.float32).astype(
+            jnp.bfloat16
+        )
+    for copy in w2_copies[0]:
+        copy.wait_recv()
+    for copy in w3_copies[0]:
+        copy.start()
+    qkv_copy.wait()
+    for c in range(chunks):
+        for copy in ag_copies[c]:
+            copy.wait()
+
+    row_ids = lax.broadcasted_iota(jnp.int32, (total, total), 0)
+    col_ids = lax.broadcasted_iota(jnp.int32, (total, total), 1)
+    seg_start = row_ids // seg_len * seg_len
+    visible = (col_ids <= row_ids) & (col_ids >= seg_start - mem_len)
+    lanes = lax.broadcasted_iota(jnp.int32, (1, cols), 1) // head_dim
+    heads = cols // head_dim
+    own_cols = pl.ds(pl.multiple_of(me * cols, cols), cols)
+    nt = (((1,), (1,)), ((), ()))
+    mx_all = []
+
+    for l in range(layers):
+        parts = []
+        for j in range(3):
+            acc = None
+            for c in range(chunks):
+                term = jnp.dot(
+                    hid[c], qkv[l, c * cw : (c + 1) * cw, j * cols : (j + 1) * cols],
+                    preferred_element_type=jnp.float32,
+                )
+                acc = term if acc is None else acc + term
+            parts.append(acc.astype(jnp.bfloat16))
+        query, key, value = parts
+        query = query.astype(jnp.float32)
+        content_q = query + cb_ref[l : l + 1, own_cols]
+        position_q = query + pb_ref[l : l + 1, own_cols]
+        mixed = jnp.zeros((total, cols), jnp.float32)
+        for h in range(heads):
+            here = lanes == h
+            cq = jnp.where(here, content_q, 0.0).astype(jnp.bfloat16)
+            pq = jnp.where(here, position_q, 0.0).astype(jnp.bfloat16)
+            content = lax.dot_general(cq, key, nt, preferred_element_type=jnp.float32)
+            raw = lax.dot_general(pq, pkeys[l], nt, preferred_element_type=jnp.float32)
+            shifted = pltpu.roll(raw, 1, 1, stride=1, stride_axis=0)
+            scores = (content + shifted) * (1.0 / math.sqrt(head_dim))
+            scores = jnp.where(visible, scores, -1e30)
+            top = jnp.max(scores, axis=1, keepdims=True)
+            weights = jnp.exp(scores - top)
+            probs = (weights * (1.0 / jnp.sum(weights, axis=1, keepdims=True))).astype(jnp.bfloat16)
+            out = jnp.dot(probs, value, preferred_element_type=jnp.float32)
+            mixed = jnp.where(here, out, mixed)
+        mixg[l, me] = mixed.astype(jnp.bfloat16)
+        mx = []
+        for k in range(1, n):
+            ref = mixg.at[l, me]
+            copy = remote(ref, ref, mx_s.at[l, k - 1], mx_r.at[l, k - 1], seg_peer(k))
+            copy.start()
+            mx.append(copy)
+        if l + 1 < layers:
+            for copy in w1_copies[l + 1]:
+                copy.wait_recv()
+            for copy in w2_copies[l + 1]:
+                copy.start()
+        if l > 0:
+            for copy in w2_copies[l]:
+                copy.wait_recv()
+            for copy in w3_copies[l]:
+                copy.start()
+        for copy in w3_copies[l]:
+            copy.wait_recv()
+        for copy in mx:
+            copy.wait()
+        for s in range(n):
+            acc = hid_cols(hid, s, cols)
+            for k in range(n):
+                acc = acc + jnp.dot(
+                    mixg[l, k], wfull[l, s, k * cols : (k + 1) * cols, :],
+                    preferred_element_type=jnp.float32,
+                )
+            xres[:, s * cols : (s + 1) * cols] = acc
+        x = xres[...]
+        mid = jnp.mean(x, axis=1, keepdims=True)
+        dev = x - mid
+        spread = jnp.mean(dev * dev, axis=1, keepdims=True)
+        normed = (
+            dev * (1.0 / jnp.sqrt(spread + EPS)) * ng_ref[l : l + 1, :] + ns_ref[l : l + 1, :]
+        ).astype(jnp.bfloat16)
+        for c in range(chunks):
+            hid[c] = normed[:, c * cw : (c + 1) * cw]
+
+    final = normed
+    top = jnp.full((total, 1), -jnp.inf, jnp.float32)
+    amount = jnp.zeros((total, 1), jnp.float32)
+    pick = jnp.zeros((total, 1), jnp.float32)
+    for v in range(vocab // wb):
+        logits = lax.dot_general(
+            final, emb[v * wb : (v + 1) * wb, :], nt, preferred_element_type=jnp.float32
+        )
+        words = lax.broadcasted_iota(jnp.int32, (total, wb), 1) + v * wb
+        newer = jnp.maximum(top, jnp.max(logits, axis=1, keepdims=True))
+        amount = amount * jnp.exp(top - newer) + jnp.sum(
+            jnp.exp(logits - newer), axis=1, keepdims=True
+        )
+        pick = pick + jnp.sum(jnp.where(words == targets, logits, 0.0), axis=1, keepdims=True)
+        top = newer
+    diag = row_ids == col_ids
+
+    def as_row(col):
+        return jnp.sum(jnp.where(diag, col, 0.0), axis=0, keepdims=True)
+
+    stats[0, 0:1, :] = as_row(top)
+    stats[0, 1:2, :] = as_row(amount)
+    stats[0, 2:3, :] = as_row(pick)
+    stats[0, 3:8, :] = jnp.zeros((5, total), jnp.float32)
+    st = [
+        remote(stats.at[0], stats.at[k], st_s.at[k - 1], st_r.at[k - 1], seg_peer(k))
+        for k in range(1, n)
+    ]
+    for copy in st:
+        copy.start()
+    for group in [id_copies] + rs_copies + w1_copies + w2_copies + w3_copies:
+        for copy in group:
+            copy.wait_send()
+    for copy in st:
+        copy.wait()
+    best = stats[0, 0:1, :]
+    for k in range(1, n):
+        best = jnp.maximum(best, stats[k, 0:1, :])
+    amount = jnp.zeros((1, total), jnp.float32)
+    pick = jnp.zeros((1, total), jnp.float32)
+    for k in range(n):
+        amount = amount + stats[k, 1:2, :] * jnp.exp(stats[k, 0:1, :] - best)
+        pick = pick + stats[k, 2:3, :]
+    loglik = pick - (jnp.log(amount) + best)
+    own = jnp.zeros((1, seg_len), jnp.float32)
+    for s in range(n):
+        own = own + jnp.where(me == s, 1.0, 0.0) * loglik[:, s * seg_len : (s + 1) * seg_len]
+    row_out[...] = jnp.broadcast_to(own, row_out.shape)
+    mean = jnp.sum(loglik, axis=1, keepdims=True) * (1.0 / total)
+    mean_out[...] = jnp.broadcast_to(mean, mean_out.shape)
+
+
+def hid_cols(hid, s, cols):
+    cw = hid.shape[2]
+    if cols == cw:
+        return hid[s].astype(jnp.float32)
+    c, at = divmod(s * cols, cw)
+    return hid[c, :, at : at + cols].astype(jnp.float32)
+
+
+def mega(
+    n, docs, tokens, targets, embedding, qkv_weight, pos_weight, out_weight,
+    content_bias, position_bias, norm_gain, norm_shift,
+):
+    seg_len = tokens.shape[0]
+    vocab, width = embedding.shape
+    layers = qkv_weight.shape[0]
+    cols = width // n
+    total = n * seg_len
+    cw = 256
+    chunks = width // cw
+    pairs = docs // 2
+    ids = jnp.broadcast_to(jnp.concatenate([tokens, targets])[None, :], (8, 2 * seg_len))
+    qkv = qkv_weight.reshape(layers, width, 3 * cols)
+    step = 16
+    inverse = jnp.power(10000.0, -jnp.arange(0, width, 2).astype(jnp.float32) / width)[None, :]
+    low = (step - 1 - jnp.arange(step)).astype(jnp.float32)[:, None] * inverse
+    high = (total - step - step * jnp.arange(total // step)).astype(jnp.float32)[:, None] * inverse
+    bf, f32 = jnp.bfloat16, jnp.float32
+    dma = pltpu.SemaphoreType.DMA
+    vmem = pl.BlockSpec(memory_space=pltpu.VMEM)
+    hbm = pl.BlockSpec(memory_space=pl.ANY)
+    row, mean = pl.pallas_call(
+        functools.partial(
+            mega_kernel, n, docs, seg_len, MEM_SEGS * seg_len, width // HEADS
+        ),
+        out_shape=(
+            jax.ShapeDtypeStruct((8, seg_len), f32),
+            jax.ShapeDtypeStruct((8, 128), f32),
+        ),
+        in_specs=[vmem, hbm, hbm, hbm, hbm] + [vmem] * 8,
+        out_specs=(vmem, vmem),
+        scratch_shapes=[
+            pltpu.VMEM((vocab, width), bf),
+            pltpu.VMEM((layers, width, 3 * cols), bf),
+            pltpu.VMEM((layers, width, cols), bf),
+            pltpu.VMEM((layers, n, width, cols), bf),
+            pltpu.VMEM((n, 8, 2 * seg_len), jnp.int32),
+            pltpu.VMEM((total, vocab), bf),
+            pltpu.VMEM((chunks, total, cw), bf),
+            pltpu.VMEM((chunks, n - 1, seg_len, cw), bf),
+            pltpu.VMEM((chunks, total, cw), bf),
+            pltpu.VMEM((total, width), bf),
+            pltpu.VMEM((layers, total, cols), bf),
+            pltpu.VMEM((layers, n, total, cols), bf),
+            pltpu.VMEM((n, 8, total), f32),
+            pltpu.VMEM((total, width), f32),
+            dma((chunks,)), dma, dma, dma((layers,)),
+            dma((n - 1,)), dma((n - 1,)),
+            dma((chunks, n - 1)), dma((chunks, n - 1)),
+            dma((chunks, n - 1)), dma((chunks, n - 1)),
+            dma((layers, n - 1)), dma((layers, n - 1)),
+            dma((layers, n - 1, pairs - 1)), dma((layers, n - 1, pairs - 1)),
+            dma((layers, n - 1, pairs)), dma((layers, n - 1, pairs)),
+            dma((layers, n - 1)), dma((layers, n - 1)),
+            dma((n - 1,)), dma((n - 1,)),
+        ],
+        compiler_params=pltpu.CompilerParams(
+            collective_id=0, has_side_effects=True, vmem_limit_bytes=60 * 1024 * 1024
+        ),
+    )(
+        ids, embedding, qkv, pos_weight, out_weight, content_bias, position_bias,
+        norm_gain, norm_shift, jnp.sin(low), jnp.cos(low), jnp.sin(high), jnp.cos(high),
+    )
+    return row[0], mean[0, :1]
+
+
+def fits_kernel(n, docs, seg_len, vocab_rows, width, layers):
+    cols = width // n
+    total = n * seg_len
+    return (
+        n > 1 and docs >= 4 and docs % 2 == 0 and cols % 128 == 0 and 256 % cols == 0
+        and width % 256 == 0 and vocab_rows % 512 == 0 and total % 128 == 0
+        and 2 * seg_len == 128 and total <= 512 and width % docs == 0
+        and (width // docs) % 16 == 0 and layers == 2
+    )
+
+
 def solution(mesh):
     in_specs = (
         P(("doc", "seg")),
@@ -214,6 +643,15 @@
         P(),
     )
     out_specs = (P(("doc", "seg")), P("doc"))
+    n, docs = mesh.shape["seg"], mesh.shape["doc"]
+
+    def body(tokens, targets, embedding, qkv_weight, *others):
+        vocab_rows, width = embedding.shape
+        layers = qkv_weight.shape[0]
+        if fits_kernel(n, docs, tokens.shape[0], vocab_rows, width, layers):
+            return mega(n, docs, tokens, targets, embedding, qkv_weight, *others)
+        return on_device(tokens, targets, embedding, qkv_weight, *others)
+
     return jax.shard_map(
-        on_device, mesh=mesh, in_specs=in_specs, out_specs=out_specs, check_vma=False
-    )
+        body, mesh=mesh, in_specs=in_specs, out_specs=out_specs, check_vma=False
+    )

time: 230 us -> 90.2 us (0.39)
  blocking collectives: 105 us -> 0 us
  Pallas kernels: 0 us -> 78.6 us
  waiting for transfers between devices: 29.9 us -> 0 us
  local copies, waits for them, and re-layouts: 37.2 us -> 8.98 us
  matrix products: 21.2 us -> 0 us
  between operations: 16.6 us -> 0.65 us
  other arithmetic: 12.3 us -> 1.71 us
  starting transfers between devices: 7.01 us -> 0 us
    all_gather x6 -> x0, blocking collectives: 84.1 us -> none  [the longest x2 43.4 us: head_attention(): piece = lax.all_gather(layer_input, 'seg', axis=0, tiled=True)]
    pallas_call x0 -> x1, Pallas kernels: none -> 78.6 us  [mega(): pl.pallas_call(functools.partial(mega_kernel, n, docs, seg_len, MEM_SEGS...]
    dot_general x13 -> x0, matrix products: 21.2 us -> none  [the longest x1 5.89 us: on_device(): jnp.einsum('td,vd->tv', lax.all_gather(hidden, 'seg', axis=0, tiled=True)...]
    all_to_all x2 -> x0, waiting for transfers between devices: 15.5 us -> none  [head_attention(): return lax.all_to_all(mixed, 'seg', split_axis=0, concat_axis=1, tiled=True)]
    psum x1 -> x0, blocking collectives: 11 us -> none  [on_device(): grand_total = lax.psum(jnp.sum(token_loglik), 'seg')]
    slice x17 -> x1, local copies, waits for them, and re-layouts: 11.3 us -> 1.19 us  [mega(): return (row[0], mean[0, :1])]
    unnamed x1 -> x0, blocking collectives: 9.92 us -> none
    reduce_scatter x1 -> x0, waiting for transfers between devices: 8.05 us -> none  [on_device(): lax.psum_scatter(jnp.where(inside[:, None], rows.astype(jnp.float32), 0.0...]
  transfers between devices with their start and end apart: 5 -> 0, of which waited for: 5 -> 0; matrix products, arithmetic and copies ran while one was open for 21% -> 0% of each run, Pallas kernels for 0% -> 0%
where the time goes in v1:
time: 90.2 us; the launch traced here: 89.9 us
  Pallas kernels  78.6 us (87%)
  local copies, waits for them, and re-layouts  8.98 us (10%)
  other arithmetic  1.71 us (2%)
    pallas_call x1, Pallas kernels, mega(): pl.pallas_call(functools.partial(mega_kernel, n, docs, seg_len, MEM_SEGS...  78.6 us
    unnamed x1, local copies, waits for them, and re-layouts  3.18 us
    reshape x1, local copies, waits for them, and re-layouts, mega(): qkv = qkv_weight.reshape(layers, width, 3 * cols)  2.82 us

profile of v1, /device:TPU:0, one launch (start us, length us, event | category | flops | bytes accessed | tf_op | source)
XLA Modules:
  0.0 89.9 jit_solution(7266533730394541917)
XLA Ops:
  0.6 0.7 pad_add_fusion
  1.4 0.6 broadcast_in_dim.2.ids_ref
  2.0 3.2 %copy.13 = bf16[2,1024,3,256]{1,3,2,0:T(8,128)(2,1)S(1)} copy(bf16[2,1024,3,256]{3,1,2,0:T(8,128)(2,1)} %param.13) | data formatting | bytes 6291456 | tf_op args[3]
  5.2 2.8 %copy.14.qkv_hbm = bf16[2,1024,768]{2,1,0:T(8,128)(2,1)} copy(bf16[2,1024,768]{1,2,0:T(8,128)(2,1)S(1)} %bitcast.4) | data formatting | bytes 6291456 | tf_op jit(solution)/shard_map/reshape | solution.py:567
  8.0 0.9 %multiply_cosine_fusion = (f32[16,512]{1,0:T(8,128)}, f32[16,512]{1,0:T(8,128)}, f32[16,512]{1,0:T(8,128)}, f32[16,512]{1,0:T(8,128)}) fusion(f32[16]{0:T(128)S(1)} %get-tuple-element.12, f32[512]{0:T(512)S(1)} %multiply_power_fusion, f32[16]{0:T(128)S(1)} %get-tuple-element.13), kind=kLoop, calls=%fused_computation | loop fusion | flops 16384 | bytes 133248 | tf_op jit(solution)/shard_map/cos | solution.py:616
  8.9 78.6 %shard_map.113 = (f32[8,64]{1,0:T(8,128)}, f32[8,128]{1,0:T(8,128)}) custom-call(s32[8,128]{1,0:T(8,128)} %broadcast_in_dim.2.ids_ref, bf16[5120,1024]{1,0:T(8,128)(2,1)} %emb_hbm.1, bf16[2,1024,768]{2,1,0:T(8,128)(2,1)} %copy.14.qkv_hbm, bf16[2,1024,256]{2,1,0:T(8,128)(2,1)} %pos_hbm.1, bf16[2,1024,256]{2,1,0:T(8,128)(2,1)} %out_hbm.1, f32[2,1024]{1,0:T(2,128)} %cb_ref.1, ...), custom_call_target="tpu_custom_call" | custom-call | tf_op jit(solution)/shard_map/pallas_call | solution.py:576
  87.5 1.2 %slice_bitcast_fusion = f32[64]{0:T(128)} fusion(f32[8,64]{1,0:T(8,128)} %get-tuple-element.4), kind=kLoop, calls=%fused_computation.6 | loop fusion | bytes 512 | tf_op jit(solution)/shard_map/squeeze | solution.py:618
  88.7 1.2 %slice.7 = f32[1,1]{1,0:T(1,128)} slice(f32[8,128]{1,0:T(8,128)} %get-tuple-element.5), slice={[0:1], [0:1]} | slice | bytes 8 | tf_op jit(solution)/shard_map/slice | solution.py:618
  (2 shorter events, 0.0 us)

commit v2 on v1

--- a/solution.py
+++ b/solution.py
@@ -209,12 +209,12 @@
 
 def mega_kernel(
     n, docs, seg_len, mem_len, head_dim,
-    ids_ref, emb_hbm, qkv_hbm, pos_hbm, out_hbm, cb_ref, pb_ref, ng_ref, ns_ref,
+    tokens_ref, targets_ref, emb_hbm, qkv_hbm, pos_hbm, out_hbm, cb_ref, pb_ref, ng_ref, ns_ref,
     lo_sin, lo_cos, hi_sin, hi_cos,
     row_out, mean_out,
-    emb, qkv, posw, wfull, idbuf, onehot, gsend, rsbuf, hid, table, pkeys, mixg, stats, xres,
+    emb, qkv, posw, wfull, idbuf, onehot, gsend, fromleft, fromright, toright, toleft, hid, table, pkeys, mixg, stats, xres,
     emb_sem, w_sem, p_sem, o_sem,
-    id_s, id_r, rs_s, rs_r, ag_s, ag_r, w1_s, w1_r, w2_s, w2_r, w3_s, w3_r, mx_s, mx_r, st_s, st_r,
+    id_s, id_r, rr_s, rr_r, rl_s, rl_r, w1_s, w1_r, w2_s, w2_r, w3_s, w3_r, mr_s, mr_r, ml_s, ml_r, st_s, st_r,
 ):
     layers = qkv.shape[0]
     total = n * seg_len
@@ -262,6 +262,9 @@
     pos_copy.start()
     qkv_copy.start()
 
+    idbuf[n - 1, 0:1, :seg_len] = tokens_ref[...]
+    idbuf[n - 1, 0:1, seg_len:] = targets_ref[...]
+    idbuf[n - 1, 1:8, :] = jnp.zeros((7, 2 * seg_len), jnp.int32)
     barrier = pltpu.get_barrier_semaphore()
     friends = [seg_peer(k) for k in range(1, n)] + [plane_peer(j) for j in range(1, pairs)]
     friends.append((partner, me))
@@ -270,7 +273,7 @@
     pl.semaphore_wait(barrier, len(friends))
 
     id_copies = [
-        remote(ids_ref, idbuf.at[k - 1], id_s.at[k - 1], id_r.at[k - 1], seg_peer(k))
+        remote(idbuf.at[n - 1], idbuf.at[k - 1], id_s.at[k - 1], id_r.at[k - 1], seg_peer(k))
         for k in range(1, n)
     ]
     for copy in id_copies:
@@ -281,14 +284,13 @@
     def w1(l):
         return [
             remote(
-                wfull.at[l, me, mine], wfull.at[l, me, mine], w1_s.at[l, k - 1],
+                out_hbm.at[l, mine], wfull.at[l, me, mine], w1_s.at[l, k - 1],
                 w1_r.at[l, k - 1], seg_peer(k),
             )
             for k in range(1, n)
         ]
 
     w1_copies = [w1(l) for l in range(layers)]
-    out_copies[0].wait()
     for copy in w1_copies[0]:
         copy.start()
 
@@ -327,7 +329,6 @@
 
     for copy in id_copies:
         copy.wait_recv()
-    idbuf[n - 1] = ids_ref[...]
     first_word = me * vocab
     tok_cols = []
     tgt_cols = []
@@ -346,28 +347,64 @@
     def rows_of(s):
         return pl.ds(pl.multiple_of(s * seg_len, seg_len), seg_len)
 
-    rs_copies = []
-    for c in range(chunks):
-        emb_copies[c].wait()
+    steps = gsend.shape[0]
+    nw = gsend.shape[2]
+    right = (doc, jnp.minimum(me + 1, n - 1))
+    left = (doc, jnp.maximum(me - 1, 0))
+
+    @pl.when(me == 0)
+    def _():
+        fromleft[...] = jnp.zeros_like(fromleft)
+
+    @pl.when(me == n - 1)
+    def _():
+        fromright[...] = jnp.zeros_like(fromright)
+
+    def chain_right(c):
+        return remote(toright.at[c], fromleft.at[c], rr_s.at[c], rr_r.at[c], right)
+
+    def chain_left(c):
+        return remote(toleft.at[c], fromright.at[c], rl_s.at[c], rl_r.at[c], left)
+
+    def advance(t):
+        cr = t - me
+
+        @pl.when((cr >= 0) & (cr < steps))
+        def _():
+            @pl.when(me > 0)
+            def _():
+                chain_right(cr).wait_recv()
+
+            @pl.when(me < n - 1)
+            def _():
+                toright[cr] = fromleft[cr] + gsend[cr]
+                chain_right(cr).start()
+
+        cl = t - (n - 1 - me)
+
+        @pl.when((cl >= 0) & (cl < steps))
+        def _():
+            @pl.when(me < n - 1)
+            def _():
+                chain_left(cl).wait_recv()
+
+            @pl.when(me > 0)
+            def _():
+                toleft[cl] = fromright[cl] + gsend[cl]
+                chain_left(cl).start()
+
+    for c in range(steps):
+        if c * nw % cw == 0:
+            emb_copies[c * nw // cw].wait()
         gsend[c] = jnp.dot(
-            onehot[...], emb[:, c * cw : (c + 1) * cw], preferred_element_type=jnp.float32
+            onehot[...], emb[:, c * nw : (c + 1) * nw], preferred_element_type=jnp.float32
         ).astype(jnp.bfloat16)
-        group = []
-        for k in range(1, n):
-            peer = lax.rem(me + k, n)
-            copy = remote(
-                gsend.at[c, rows_of(peer)], rsbuf.at[c, k - 1], rs_s.at[c, k - 1],
-                rs_r.at[c, k - 1], (doc, peer),
-            )
-            copy.start()
-            group.append(copy)
-        rs_copies.append(group)
+        advance(c)
 
     for copy in w1_copies[0]:
         copy.wait_recv()
     for copy in w2_copies[0]:
         copy.start()
-    out_copies[1].wait()
 
     step = lo_sin.shape[0]
     half = width // 2
@@ -378,22 +415,7 @@
         table[rows, :half] = (hs * lo_cos[...] + hc * lo_sin[...]).astype(jnp.bfloat16)
         table[rows, half:] = (hc * lo_cos[...] - hs * lo_sin[...]).astype(jnp.bfloat16)
 
-    ag_copies = []
-    for c in range(chunks):
-        for copy in rs_copies[c]:
-            copy.wait_recv()
-        own = gsend[c, rows_of(me), :].astype(jnp.float32)
-        for k in range(1, n):
-            own = own + rsbuf[c, k - 1].astype(jnp.float32)
-        hid[c, rows_of(me), :] = (own * math.sqrt(width)).astype(jnp.bfloat16)
-        group = []
-        for k in range(1, n):
-            ref = hid.at[c, rows_of(me)]
-            copy = remote(ref, ref, ag_s.at[c, k - 1], ag_r.at[c, k - 1], seg_peer(k))
-            copy.start()
-            group.append(copy)
-        ag_copies.append(group)
-
+    pl.loop(steps, steps + n - 1)(advance)
     for l in range(1, layers):
         for copy in w1_copies[l]:
             copy.start()
@@ -408,10 +430,48 @@
     for copy in w3_copies[0]:
         copy.start()
     qkv_copy.wait()
-    for c in range(chunks):
-        for copy in ag_copies[c]:
-            copy.wait()
-
+    for c in range(steps):
+        looked = fromleft[c].astype(jnp.float32) + gsend[c].astype(jnp.float32)
+        looked = (looked + fromright[c].astype(jnp.float32)) * math.sqrt(width)
+        at = c * nw % cw
+        hid[c * nw // cw, :, at : at + nw] = looked.astype(jnp.bfloat16)
+
+    def move_right(l, j, b, src):
+        ref = mixg.at[l, jnp.maximum(src, 0), b * rb : (b + 1) * rb]
+        return remote(ref, ref, mr_s.at[l, j, b], mr_r.at[l, j, b], right)
+
+    def move_left(l, j, b, src):
+        ref = mixg.at[l, jnp.minimum(src, n - 1), b * rb : (b + 1) * rb]
+        return remote(ref, ref, ml_s.at[l, j, b], ml_r.at[l, j, b], left)
+
+    def each_way(l, j, b, part):
+        if part == "start" or part == "sent":
+            act_r = (me - j >= 0) & (me < n - 1)
+            act_l = (me + j < n) & (me > 0)
+            at_r, at_l = me - j, me + j
+        else:
+            act_r = me - 1 - j >= 0
+            act_l = me + 1 + j < n
+            at_r, at_l = me - 1 - j, me + 1 + j
+
+        def act(copy):
+            if part == "start":
+                copy.start()
+            elif part == "sent":
+                copy.wait_send()
+            else:
+                copy.wait_recv()
+
+        @pl.when(act_r)
+        def _():
+            act(move_right(l, j, b, at_r))
+
+        @pl.when(act_l)
+        def _():
+            act(move_left(l, j, b, at_l))
+
+    halves = mr_s.shape[2]
+    rb = total // halves
     row_ids = lax.broadcasted_iota(jnp.int32, (total, total), 0)
     col_ids = lax.broadcasted_iota(jnp.int32, (total, total), 1)
     seg_start = row_ids // seg_len * seg_len
@@ -420,7 +480,6 @@
     heads = cols // head_dim
     own_cols = pl.ds(pl.multiple_of(me * cols, cols), cols)
     nt = (((1,), (1,)), ((), ()))
-    mx_all = []
 
     for l in range(layers):
         parts = []
@@ -428,7 +487,7 @@
             acc = None
             for c in range(chunks):
                 term = jnp.dot(
-                    hid[c], qkv[l, c * cw : (c + 1) * cw, j * cols : (j + 1) * cols],
+                    hid[c], qkv[l, j, c * cw : (c + 1) * cw, :],
                     preferred_element_type=jnp.float32,
                 )
                 acc = term if acc is None else acc + term
@@ -437,28 +496,32 @@
         query = query.astype(jnp.float32)
         content_q = query + cb_ref[l : l + 1, own_cols]
         position_q = query + pb_ref[l : l + 1, own_cols]
-        mixed = jnp.zeros((total, cols), jnp.float32)
-        for h in range(heads):
-            here = lanes == h
-            cq = jnp.where(here, content_q, 0.0).astype(jnp.bfloat16)
-            pq = jnp.where(here, position_q, 0.0).astype(jnp.bfloat16)
-            content = lax.dot_general(cq, key, nt, preferred_element_type=jnp.float32)
-            raw = lax.dot_general(pq, pkeys[l], nt, preferred_element_type=jnp.float32)
-            shifted = pltpu.roll(raw, 1, 1, stride=1, stride_axis=0)
-            scores = (content + shifted) * (1.0 / math.sqrt(head_dim))
-            scores = jnp.where(visible, scores, -1e30)
-            top = jnp.max(scores, axis=1, keepdims=True)
-            weights = jnp.exp(scores - top)
-            probs = (weights * (1.0 / jnp.sum(weights, axis=1, keepdims=True))).astype(jnp.bfloat16)
-            out = jnp.dot(probs, value, preferred_element_type=jnp.float32)
-            mixed = jnp.where(here, out, mixed)
-        mixg[l, me] = mixed.astype(jnp.bfloat16)
-        mx = []
-        for k in range(1, n):
-            ref = mixg.at[l, me]
-            copy = remote(ref, ref, mx_s.at[l, k - 1], mx_r.at[l, k - 1], seg_peer(k))
-            copy.start()
-            mx.append(copy)
+        for b in range(halves):
+            rows = slice(b * rb, (b + 1) * rb)
+            span = (b + 1) * rb
+            mixed = jnp.zeros((rb, cols), jnp.float32)
+            for h in range(heads):
+                here = lanes == h
+                cq = jnp.where(here, content_q[rows], 0.0).astype(jnp.bfloat16)
+                pq = jnp.where(here, position_q[rows], 0.0).astype(jnp.bfloat16)
+                content = lax.dot_general(cq, key[:span], nt, preferred_element_type=jnp.float32)
+                raw = lax.dot_general(pq, pkeys[l], nt, preferred_element_type=jnp.float32)
+                shifted = pltpu.roll(raw, b * rb + 1, 1, stride=1, stride_axis=0)[:, :span]
+                scores = (content + shifted) * (1.0 / math.sqrt(head_dim))
+                scores = jnp.where(visible[rows, :span], scores, -1e30)
+                top = jnp.max(scores, axis=1, keepdims=True)
+                weights = jnp.exp(scores - top)
+                probs = (weights * (1.0 / jnp.sum(weights, axis=1, keepdims=True))).astype(
+                    jnp.bfloat16
+                )
+                out = jnp.dot(probs, value[:span], preferred_element_type=jnp.float32)
+                mixed = jnp.where(here, out, mixed)
+            mixg[l, me, rows, :] = mixed.astype(jnp.bfloat16)
+            each_way(l, 0, b, "start")
+        for j in range(1, n - 1):
+            for b in range(halves):
+                each_way(l, j - 1, b, "got")
+                each_way(l, j, b, "start")
         if l + 1 < layers:
             for copy in w1_copies[l + 1]:
                 copy.wait_recv()
@@ -471,23 +534,30 @@
                 copy.start()
         for copy in w3_copies[l]:
             copy.wait_recv()
-        for copy in mx:
-            copy.wait()
-        for s in range(n):
-            acc = hid_cols(hid, s, cols)
-            for k in range(n):
-                acc = acc + jnp.dot(
-                    mixg[l, k], wfull[l, s, k * cols : (k + 1) * cols, :],
-                    preferred_element_type=jnp.float32,
-                )
-            xres[:, s * cols : (s + 1) * cols] = acc
-        x = xres[...]
-        mid = jnp.mean(x, axis=1, keepdims=True)
-        dev = x - mid
-        spread = jnp.mean(dev * dev, axis=1, keepdims=True)
-        normed = (
-            dev * (1.0 / jnp.sqrt(spread + EPS)) * ng_ref[l : l + 1, :] + ns_ref[l : l + 1, :]
-        ).astype(jnp.bfloat16)
+        out_copies[l].wait()
+        normed = []
+        for b in range(halves):
+            rows = slice(b * rb, (b + 1) * rb)
+            each_way(l, n - 2, b, "got")
+            for s in range(n):
+                acc = hid_cols(hid, s, cols)[rows]
+                for k in range(n):
+                    acc = acc + jnp.dot(
+                        mixg[l, k, rows, :], wfull[l, s, k * cols : (k + 1) * cols, :],
+                        preferred_element_type=jnp.float32,
+                    )
+                xres[rows, s * cols : (s + 1) * cols] = acc
+            x = xres[rows, :]
+            mid = jnp.mean(x, axis=1, keepdims=True)
+            dev = x - mid
+            spread = jnp.mean(dev * dev, axis=1, keepdims=True)
+            normed.append(
+                (
+                    dev * (1.0 / jnp.sqrt(spread + EPS)) * ng_ref[l : l + 1, :]
+                    + ns_ref[l : l + 1, :]
+                ).astype(jnp.bfloat16)
+            )
+        normed = jnp.concatenate(normed, axis=0)
         for c in range(chunks):
             hid[c] = normed[:, c * cw : (c + 1) * cw]
 
@@ -521,7 +591,20 @@
     ]
     for copy in st:
         copy.start()
-    for group in [id_copies] + rs_copies + w1_copies + w2_copies + w3_copies:
+    for c in range(steps):
+        @pl.when(me < n - 1)
+        def _():
+            chain_right(c).wait_send()
+
+        @pl.when(me > 0)
+        def _():
+            chain_left(c).wait_send()
+
+    for l in range(layers):
+        for j in range(n - 1):
+            for b in range(halves):
+                each_way(l, j, b, "sent")
+    for group in [id_copies] + w1_copies + w2_copies + w3_copies:
         for copy in group:
             copy.wait_send()
     for copy in st:
@@ -538,9 +621,9 @@
     own = jnp.zeros((1, seg_len), jnp.float32)
     for s in range(n):
         own = own + jnp.where(me == s, 1.0, 0.0) * loglik[:, s * seg_len : (s + 1) * seg_len]
-    row_out[...] = jnp.broadcast_to(own, row_out.shape)
+    row_out[...] = own
     mean = jnp.sum(loglik, axis=1, keepdims=True) * (1.0 / total)
-    mean_out[...] = jnp.broadcast_to(mean, mean_out.shape)
+    mean_out[...] = mean
 
 
 def hid_cols(hid, s, cols):
@@ -562,9 +645,10 @@
     total = n * seg_len
     cw = 256
     chunks = width // cw
+    nw = 128
+    steps = width // nw
     pairs = docs // 2
-    ids = jnp.broadcast_to(jnp.concatenate([tokens, targets])[None, :], (8, 2 * seg_len))
-    qkv = qkv_weight.reshape(layers, width, 3 * cols)
+    qkv = qkv_weight.transpose(0, 2, 1, 3)
     step = 16
     inverse = jnp.power(10000.0, -jnp.arange(0, width, 2).astype(jnp.float32) / width)[None, :]
     low = (step - 1 - jnp.arange(step)).astype(jnp.float32)[:, None] * inverse
@@ -578,20 +662,23 @@
             mega_kernel, n, docs, seg_len, MEM_SEGS * seg_len, width // HEADS
         ),
         out_shape=(
-            jax.ShapeDtypeStruct((8, seg_len), f32),
-            jax.ShapeDtypeStruct((8, 128), f32),
+            jax.ShapeDtypeStruct((1, seg_len), f32),
+            jax.ShapeDtypeStruct((1, 1), f32),
         ),
-        in_specs=[vmem, hbm, hbm, hbm, hbm] + [vmem] * 8,
+        in_specs=[vmem] * 2 + [hbm] * 4 + [vmem] * 8,
         out_specs=(vmem, vmem),
         scratch_shapes=[
             pltpu.VMEM((vocab, width), bf),
-            pltpu.VMEM((layers, width, 3 * cols), bf),
+            pltpu.VMEM((layers, 3, width, cols), bf),
             pltpu.VMEM((layers, width, cols), bf),
             pltpu.VMEM((layers, n, width, cols), bf),
             pltpu.VMEM((n, 8, 2 * seg_len), jnp.int32),
             pltpu.VMEM((total, vocab), bf),
-            pltpu.VMEM((chunks, total, cw), bf),
-            pltpu.VMEM((chunks, n - 1, seg_len, cw), bf),
+            pltpu.VMEM((steps, total, nw), bf),
+            pltpu.VMEM((steps, total, nw), bf),
+            pltpu.VMEM((steps, total, nw), bf),
+            pltpu.VMEM((steps, total, nw), bf),
+            pltpu.VMEM((steps, total, nw), bf),
             pltpu.VMEM((chunks, total, cw), bf),
             pltpu.VMEM((total, width), bf),
             pltpu.VMEM((layers, total, cols), bf),
@@ -600,22 +687,22 @@
             pltpu.VMEM((total, width), f32),
             dma((chunks,)), dma, dma, dma((layers,)),
             dma((n - 1,)), dma((n - 1,)),
-            dma((chunks, n - 1)), dma((chunks, n - 1)),
-            dma((chunks, n - 1)), dma((chunks, n - 1)),
+            dma((steps,)), dma((steps,)), dma((steps,)), dma((steps,)),
             dma((layers, n - 1)), dma((layers, n - 1)),
             dma((layers, n - 1, pairs - 1)), dma((layers, n - 1, pairs - 1)),
             dma((layers, n - 1, pairs)), dma((layers, n - 1, pairs)),
-            dma((layers, n - 1)), dma((layers, n - 1)),
+            dma((layers, n - 1, 2)), dma((layers, n - 1, 2)),
+            dma((layers, n - 1, 2)), dma((layers, n - 1, 2)),
             dma((n - 1,)), dma((n - 1,)),
         ],
         compiler_params=pltpu.CompilerParams(
             collective_id=0, has_side_effects=True, vmem_limit_bytes=60 * 1024 * 1024
         ),
     )(
-        ids, embedding, qkv, pos_weight, out_weight, content_bias, position_bias,
+        tokens[None, :], targets[None, :], embedding, qkv, pos_weight, out_weight, content_bias, position_bias,
         norm_gain, norm_shift, jnp.sin(low), jnp.cos(low), jnp.sin(high), jnp.cos(high),
     )
-    return row[0], mean[0, :1]
+    return row.reshape(seg_len), mean.reshape(1)
 
 
 def fits_kernel(n, docs, seg_len, vocab_rows, width, layers):

time: 90.2 us -> 89.3 us (0.990)
  local copies, waits for them, and re-layouts: 8.98 us -> 1.14 us
  Pallas kernels: 78.6 us -> 84.6 us
  between operations: 0.65 us -> 2.4 us
    pallas_call x1, Pallas kernels: 78.6 us -> 84.6 us  [mega(): pl.pallas_call(functools.partial(mega_kernel, n, docs, seg_len, MEM_SEGS...]
    reshape x1 -> x0, local copies, waits for them, and re-layouts: 2.82 us -> none  [mega(): qkv = qkv_weight.reshape(layers, width, 3 * cols)]
    unnamed x1, local copies, waits for them, and re-layouts: 3.18 us -> 1.14 us
    squeeze x1 -> x0, local copies, waits for them, and re-layouts: 1.19 us -> none  [mega(): return (row[0], mean[0, :1])]
    slice x1 -> x0, local copies, waits for them, and re-layouts: 1.19 us -> none  [mega(): return (row[0], mean[0, :1])]
where the time goes in v2:
time: 89.3 us; the launch traced here: 89.1 us
  Pallas kernels  84.6 us (95%)
  between operations  2.4 us (3%)
  local copies, waits for them, and re-layouts  1.14 us (1%)
  other arithmetic  0.96 us (1%)
    pallas_call x1, Pallas kernels, mega(): pl.pallas_call(functools.partial(mega_kernel, n, docs, seg_len, MEM_SEGS...  84.6 us

profile of v2, /device:TPU:0, one launch (start us, length us, event | category | flops | bytes accessed | tf_op | source)
XLA Modules:
  0.0 89.1 jit_solution(6738714335302917834)
XLA Ops:
  0.7 0.9 %multiply_cosine_fusion = (f32[16,512]{1,0:T(8,128)}, f32[16,512]{1,0:T(8,128)}, f32[16,512]{1,0:T(8,128)}, f32[16,512]{1,0:T(8,128)}) fusion(f32[16]{0:T(128)S(1)} %get-tuple-element.12, f32[512]{0:T(512)S(1)} %multiply_power_fusion, f32[16]{0:T(128)S(1)} %get-tuple-element.13), kind=kLoop, calls=%fused_computation | loop fusion | flops 16384 | bytes 133248 | tf_op jit(solution)/shard_map/cos | solution.py:703
  1.6 84.6 %shard_map.113 = (f32[1,64]{1,0:T(1,128)}, f32[1,1]{1,0:T(1,128)}) custom-call(s32[1,64]{1,0:T(1,128)} %bitcast.6, s32[1,64]{1,0:T(1,128)} %bitcast.7, bf16[5120,1024]{1,0:T(8,128)(2,1)} %emb_hbm.1, bf16[2,3,1024,256]{3,2,1,0:T(8,128)(2,1)} %bitcast.5, bf16[2,1024,256]{2,1,0:T(8,128)(2,1)} %pos_hbm.1, bf16[2,1024,256]{2,1,0:T(8,128)(2,1)} %out_hbm.1, ...), custom_call_target="tpu_custom_call" | custom-call | tf_op jit(solution)/shard_map/pallas_call | solution.py:660
  86.2 1.1 %copy.14 = f32[64]{0:T(128)} copy(f32[64]{0:T(128)} %bitcast.8) | data formatting | bytes 512
  (2 shorter events, 0.0 us)
